TPU v7x, 32 devices: a whole 2x2x4 slice. The times are simulated.
32 devices in a mesh: groups: 2 (over x), ctx: 16 (over z, y, core).
Axes of the slice: x: 2, y: 2, z: 4, core: 2. Of those that a mesh axis runs over, the one named last changes fastest.
Arguments:
- queries: bfloat16 [96, 4096], P(('groups', 'ctx')), parts along dimension 0, may hold values from -200 to 200
- cache_keys: bfloat16 [4096, 512], P(('groups', 'ctx')), parts along dimension 0, may hold values from -6 to 6
- cache_values: bfloat16 [4096, 512], P(('groups', 'ctx')), parts along dimension 0, may hold values from -6 to 6
- new_keys: bfloat16 [96, 512], P(('groups', 'ctx')), parts along dimension 0, may hold values from -6 to 6
- new_values: bfloat16 [96, 512], P(('groups', 'ctx')), parts along dimension 0, may hold values from -6 to 6
- cache_lengths: int32 [32], P(('groups', 'ctx')), parts along dimension 0, may hold values from 0 to 128, as said below
- residual_in: bfloat16 [96, 2048], P(('groups', 'ctx')), parts along dimension 0, may hold values from -6 to 6
- out_weight: bfloat16 [4096, 2048], P('ctx'), may hold values from -3 to 3
- norm_gain: bfloat16 [2048], replicated, may hold values from 0.25 to 1.75
- expert_gate: bfloat16 [16, 2048, 768], P('ctx'), may hold values from -0.125 to 0.125
- expert_up: bfloat16 [16, 2048, 768], P('ctx'), may hold values from -0.125 to 0.125
- expert_down: bfloat16 [16, 768, 2048], P('ctx'), may hold values from -0.21875 to 0.21875
- expert_ids: int32 [96, 8], P(('groups', 'ctx')), parts along dimension 0, may hold values from 0 to 15, all different within a row; in each aligned block of 3 rows (0 to 2, 3 to 5, ...) at most 3 rows name the same one
- expert_weights: float32 [96, 8], P(('groups', 'ctx')), parts along dimension 0, may hold values from 0.03 to 0.4
Outputs:
- layer_out: bfloat16 [96, 2048], P(('groups', 'ctx')), parts along dimension 0
There are 2 independent parts, one for each index of `groups`. A program takes and returns all parts, laid end to end along the dimension named above; an argument that names none is the same for every part. Nothing has to cross between parts.
Inputs may be any that keep to these rules, and one draw needn't show every extreme that they name: `cache_lengths`: some shard in every draw is full, with 128 live positions. `expert_ids`: within one block of 3 rows no expert is named more than 3 times, a bound that some block reaches.
All inputs are finite; a program needn't handle non-finite values.
Results may differ from a plain program's by a relative error of at most 0.01.
Values may be sent and summed in bfloat16 or wider, within the bound.
No kernel may reach another device: no remote copies, remote signals or barrier semaphores. Data moves between devices by JAX's collectives and lax.ppermute only.
A program may use at most 64 MiB of HBM per device.

v0:
```python
import jax
import jax.numpy as jnp
from jax import lax
from jax.sharding import PartitionSpec as P

HEADS = 32
KV_HEADS = 4
HEAD_DIM = 128
TOP = 8
MASKED = -1e30
epsilon = 1e-06


def local(
    queries,
    cache_keys,
    cache_values,
    new_keys,
    new_values,
    cache_lengths,
    residual_in,
    out_weight,
    norm_gain,
    expert_gate,
    expert_up,
    expert_down,
    expert_ids,
    expert_weights,
):
    shards = lax.axis_size("ctx")
    device = lax.axis_index("ctx")
    rows_dev = residual_in.shape[0]
    capacity = max(2, 2 * rows_dev * TOP // shards)
    group_size = HEADS // KV_HEADS
    whole_queries = lax.all_gather(queries, "ctx", axis=0, tiled=True)
    all_rows = whole_queries.shape[0]
    query_heads = whole_queries.reshape(all_rows, KV_HEADS, group_size, HEAD_DIM)
    local_cache = cache_keys.shape[0]
    key_rows = jnp.concatenate([cache_keys, new_keys], 0).reshape(
        local_cache + rows_dev, KV_HEADS, HEAD_DIM
    )
    value_rows = jnp.concatenate([cache_values, new_values], 0).reshape(
        local_cache + rows_dev, KV_HEADS, HEAD_DIM
    )
    slot_ids = jnp.arange(local_cache + rows_dev, dtype=jnp.int32)
    span_pos = device * rows_dev + slot_ids - local_cache
    row_ids = jnp.arange(all_rows, dtype=jnp.int32)
    usable = jnp.where(
        slot_ids[None, :] < local_cache,
        (slot_ids < cache_lengths[0])[None, :],
        span_pos[None, :] <= row_ids[:, None],
    )
    scores = jnp.einsum(
        "rkgd,nkd->kgrn", query_heads, key_rows, preferred_element_type=jnp.float32
    ) * HEAD_DIM ** (-0.5)
    scores = jnp.where(usable, scores, MASKED)
    maxima = jnp.max(scores, axis=-1)
    exp_weights = jnp.where(usable, jnp.exp(scores - maxima[..., None]), 0.0)
    totals = jnp.sum(exp_weights, axis=-1)
    numerators = jnp.einsum(
        "kgrn,nkd->rkgd",
        exp_weights.astype(jnp.bfloat16),
        value_rows,
        preferred_element_type=jnp.float32,
    ).reshape(all_rows, HEADS, HEAD_DIM)
    maxima = maxima.transpose(2, 0, 1).reshape(all_rows, HEADS)
    totals = totals.transpose(2, 0, 1).reshape(all_rows, HEADS)
    largest = lax.pmax(maxima, "ctx")
    rescale = jnp.exp(maxima - largest)
    denoms = lax.psum(totals * rescale, "ctx")
    weighted = (numerators * (rescale / denoms)[..., None]).reshape(all_rows, HEADS * HEAD_DIM)
    columns = lax.psum_scatter(weighted, "ctx", scatter_dimension=1, tiled=True).astype(
        jnp.bfloat16
    )
    projected = lax.psum_scatter(
        jnp.dot(columns, out_weight, preferred_element_type=jnp.float32),
        "ctx",
        scatter_dimension=0,
        tiled=True,
    )
    state = residual_in.astype(jnp.float32) + projected
    normed = (
        state
        * lax.rsqrt(jnp.mean(state * state, axis=1, keepdims=True) + epsilon)
        * norm_gain.astype(jnp.float32)
    ).astype(jnp.bfloat16)
    n_slots = shards * capacity
    flat_ids = expert_ids.reshape(-1)
    places = jnp.arange(flat_ids.shape[0], dtype=jnp.int32)
    earlier = (flat_ids[:, None] == flat_ids[None, :]) & (places[None, :] < places[:, None])
    slot_of = flat_ids * capacity + jnp.sum(earlier.astype(jnp.int32), axis=1)
    one_hot = (slot_of[:, None] == jnp.arange(n_slots, dtype=jnp.int32)[None, :]).astype(
        jnp.float32
    )
    dispatch_map = one_hot.reshape(rows_dev, TOP, n_slots).sum(1)
    outgoing = (
        jnp.dot(dispatch_map.T.astype(jnp.bfloat16), normed, preferred_element_type=jnp.float32)
        .astype(jnp.bfloat16)
        .reshape(shards, capacity, normed.shape[1])
    )
    received = lax.all_to_all(outgoing, "ctx", split_axis=0, concat_axis=0, tiled=True)
    gate_out = jnp.einsum(
        "scd,df->scf", received, expert_gate[0], preferred_element_type=jnp.float32
    )
    up_out = jnp.einsum("scd,df->scf", received, expert_up[0], preferred_element_type=jnp.float32)
    activated = (jax.nn.silu(gate_out) * up_out).astype(jnp.bfloat16)
    expert_out = jnp.einsum(
        "scf,fd->scd", activated, expert_down[0], preferred_element_type=jnp.float32
    ).astype(jnp.bfloat16)
    back = lax.all_to_all(expert_out, "ctx", split_axis=0, concat_axis=0, tiled=True)
    combine_map = (
        (one_hot * expert_weights.reshape(-1)[:, None]).reshape(rows_dev, TOP, n_slots).sum(1)
    )
    expert_sum = jnp.dot(
        combine_map,
        back.reshape(n_slots, normed.shape[1]).astype(jnp.float32),
        precision=lax.Precision.HIGHEST,
    )
    return (state + expert_sum).astype(jnp.bfloat16)


def solution(mesh):
    placed = (
        P(("groups", "ctx"), None),
        P(("groups", "ctx"), None),
        P(("groups", "ctx"), None),
        P(("groups", "ctx"), None),
        P(("groups", "ctx"), None),
        P(("groups", "ctx")),
        P(("groups", "ctx"), None),
        P("ctx", None),
        P(),
        P("ctx", None, None),
        P("ctx", None, None),
        P("ctx", None, None),
        P(("groups", "ctx"), None),
        P(("groups", "ctx"), None),
    )
    return jax.shard_map(
        local, mesh=mesh, in_specs=placed, out_specs=P(("groups", "ctx"), None), check_vma=False
    )
```

profile of v0, /device:TPU:0, one launch (start us, length us, event | category | flops | bytes accessed | tf_op | source)
XLA Modules:
  0.0 359.6 jit_solution(11415697979822261193)
XLA Ops:
  7.3 0.6 add_add_fusion
  7.9 0.6 iota_compare_fusion.3
  8.5 0.9 pad_maximum_fusion.1
  9.5 0.9 pad_maximum_fusion
  10.5 0.1 reshape.87
  10.6 26.4 %all-gather = bf16[16,3,4096]{2,1,0:T(4,128)(2,1)} all-gather(bf16[1,3,4096]{2,1,0:T(4,128)(2,1)} %bitcast.55), channel_id=1, replica_groups=mesh['groups'=2,'ctx'=16] {'ctx'}, dimensions={0}, use_global_device_ids=true | all-gather | bytes 417792 | tf_op jit(solution)/shard_map/all_gather | solution.py:35
  37.0 2.2 reshape.89
  39.2 0.7 fusion.36
  39.9 2.6 fusion.46
  42.5 57.8 %pmax.7 = f32[48,32]{0,1:T(8,128)S(1)} all-reduce(f32[48,32]{0,1:T(8,128)S(1)} %bitcast.53), channel_id=1, replica_groups=mesh['groups'=2,'ctx'=16] {'ctx'}, use_global_device_ids=true, to_apply=%region_1.2 | all-reduce | flops 1536 | bytes 12288 | tf_op jit(solution)/shard_map/pmax | solution.py:68
  100.3 2.1 fusion.10
  102.3 0.4 convolution_bitcast_fusion
  102.8 1.1 copy.35
  103.9 57.6 %psum.7 = f32[48,32]{0,1:T(8,128)S(1)} all-reduce(f32[48,32]{0,1:T(8,128)S(1)} %bitcast_multiply_fusion.1), channel_id=1, replica_groups=mesh['groups'=2,'ctx'=16] {'ctx'}, use_global_device_ids=true, to_apply=%region_3.4 | all-reduce | flops 1536 | bytes 12288 | tf_op jit(solution)/shard_map/psum | solution.py:70
  161.7 0.3 mul.72
  161.9 3.1 bitcast_multiply_fusion
  165.2 0.2 convert_reduce_fusion.1
  165.5 53.7 %reduce-scatter.2.cloned.1.call-done = f32[48,256]{1,0:T(8,128)} async-done(((f32[48,4096]{1,0:T(8,128)}), f32[48,256]{1,0:T(8,128)}) %reduce-scatter.2.cloned.1.call-update) | async-done | bytes 49168 | tf_op jit(solution)/shard_map/reduce_scatter | solution.py:72
  219.2 2.3 fusion.37
  221.6 0.6 dynamic-slice
  222.8 0.7 convert_reduce_fusion
  223.5 89.5 %all-reduce.3.cloned.1.call-done = f32[48,2048]{1,0:T(8,128)} async-done(((f32[48,2048]{1,0:T(8,128)}), f32[48,2048]{1,0:T(8,128)}) %all-reduce.3.cloned.1.call-update) | async-done | bytes 393232
  313.0 1.0 multiply_reduce_fusion
  314.0 1.2 convolution_convert_fusion
  315.2 0.8 reshape.93
  316.0 13.8 %all_to_all.10 = bf16[16,3,2048]{2,1,0:T(4,128)(2,1)S(1)} all-to-all(bf16[16,3,2048]{2,1,0:T(4,128)(2,1)} %reshape.93), channel_id=1, replica_groups=mesh['groups'=2,'ctx'=16] {'ctx'}, dimensions={0} | all-to-all | bytes 393216 | tf_op jit(solution)/shard_map/all_to_all | solution.py:101
  329.8 2.6 fusion.4
  332.4 3.9 %fusion.6 = bf16[16,3,2048]{2,0,1:T(8,128)(2,1)} fusion(bf16[1,768,2048]{2,1,0:T(8,128)(2,1)S(1)} %copy-done, bf16[1,2048,768]{2,1,0:T(8,128)(2,1)} %param.24, f32[16,3,768]{2,0,1:T(8,128)S(1)} %fusion.4, bf16[16,3,2048]{2,1,0:T(4,128)(2,1)S(1)} %all_to_all.10), kind=kOutput, calls=%fused_computation.6 | convolution fusion | flops 302309376 | bytes 6832128 | tf_op jit(solution)/shard_map/scf,fd->scd/dot_general | solution.py:107
  336.3 1.1 copy.39
  337.4 12.7 %all_to_all.11 = bf16[16,3,2048]{2,1,0:T(4,128)(2,1)S(1)} all-to-all(bf16[16,3,2048]{2,1,0:T(4,128)(2,1)S(1)} %copy.39), channel_id=1, replica_groups=mesh['groups'=2,'ctx'=16] {'ctx'}, dimensions={0} | all-to-all | bytes 393216 | tf_op jit(solution)/shard_map/all_to_all | solution.py:110
  350.1 0.8 reshape.94
  351.0 1.8 fusion.9
  (27 shorter events, 0.5 us)
Async XLA Ops:
  6.5 325.9 %copy-start = (bf16[1,768,2048]{2,1,0:T(8,128)(2,1)S(1)}, bf16[1,768,2048]{2,1,0:T(8,128)(2,1)}, u32[]{:S(2)}) copy-start(bf16[1,768,2048]{2,1,0:T(8,128)(2,1)} %param.25) | copy-start | bytes 9437188
  6.5 212.7 %reduce-scatter.2.cloned.1.call-start = ((), (), s32[]{:S(2)}) async-start(), calls=%async_computation.3 | async-start | bytes 835584 | tf_op jit(solution)/shard_map/reduce_scatter | solution.py:72
  100.3 2.1 copy-start.1
  161.9 3.2 copy-start.3
  165.0 56.5 %copy-start.4 = (bf16[2048]{0:T(1024)(128)(2,1)S(1)}, bf16[2048]{0:T(1024)(128)(2,1)}, u32[]{:S(2)}) copy-start(bf16[2048]{0:T(1024)(128)(2,1)} %param.22) | copy-start | bytes 12292
  165.0 56.5 %copy-start.6 = (u32[32]{0:T(128)S(1)}, u32[32]{0:T(128)}, u32[]{:S(2)}) copy-start(u32[32]{0:T(128)} %constant.43) | copy-start | bytes 388
  165.0 57.8 %copy-start.5 = (f32[3,8]{1,0:T(4,128)S(1)}, f32[3,8]{1,0:T(4,128)}, u32[]{:S(2)}) copy-start(f32[3,8]{1,0:T(4,128)} %param.27) | copy-start | bytes 292
  165.0 147.9 %copy-start.2 = (bf16[3,2048]{1,0:T(4,128)(2,1)S(1)}, bf16[3,2048]{1,0:T(4,128)(2,1)}, u32[]{:S(2)}) copy-start(bf16[3,2048]{1,0:T(4,128)(2,1)} %param.20) | copy-start | bytes 36868
  165.1 147.9 %all-reduce.3.cloned.1.call-start = ((), (), s32[]{:S(2)}) async-start(), calls=%async_computation.4 | async-start | bytes 786432
Sparse Core Ops, SparseCore 0:
  165.2 53.9 reduce-scatter.1
  222.5 90.3 all-reduce.2
where the time goes:
time: 360 us
  blocking collectives  168 us (47%)
  waiting for transfers between devices  143 us (40%)
  between operations  15 us (4%)
  matrix products  14.8 us (4%)
  other arithmetic  10.8 us (3%)
  local copies, waits for them, and re-layouts  7.41 us (2%)
    unnamed x3, waiting for transfers between devices  89.5 us
    pmax x1, blocking collectives, local(): largest = lax.pmax(maxima, 'ctx')  57.8 us
    psum x1, blocking collectives, local(): denoms = lax.psum(totals * rescale, 'ctx')  57.6 us
    reduce_scatter x1, waiting for transfers between devices, local(): lax.psum_scatter(weighted, 'ctx', scatter_dimension=1, tiled=True)  53.7 us
    all_gather x1, blocking collectives, local(): whole_queries = lax.all_gather(queries, 'ctx', axis=0, tiled=True)  26.4 us
    all_to_all x1, blocking collectives, local(): lax.all_to_all(outgoing, 'ctx', split_axis=0, concat_axis=0, tiled=True)  13.8 us
    all_to_all x1, blocking collectives, local(): lax.all_to_all(expert_out, 'ctx', split_axis=0, concat_axis=0, tiled=True)  12.7 us
  transfers between devices with their start and end apart: 2, of which 2 were waited for; matrix products, arithmetic and copies ran while one was open for 0% of the time, Pallas kernels for 0%

commit v1 on v0

--- a/solution.py
+++ b/solution.py
@@ -67,7 +67,7 @@
     totals = totals.transpose(2, 0, 1).reshape(all_rows, HEADS)
     largest = lax.pmax(maxima, "ctx")
     rescale = jnp.exp(maxima - largest)
-    denoms = lax.psum(totals * rescale, "ctx")
+    denoms = jnp.sum(lax.all_gather(totals * rescale, "ctx"), axis=0)
     weighted = (numerators * (rescale / denoms)[..., None]).reshape(all_rows, HEADS * HEAD_DIM)
     columns = lax.psum_scatter(weighted, "ctx", scatter_dimension=1, tiled=True).astype(
         jnp.bfloat16

time: 360 us -> 321 us (0.89)
  blocking collectives: 168 us -> 129 us
    psum x1 -> x0, blocking collectives: 57.6 us -> none  [local(): denoms = lax.psum(totals * rescale, 'ctx')]
    all_gather x0 -> x1, blocking collectives: none -> 17.8 us  [local(): denoms = jnp.sum(lax.all_gather(totals * rescale, 'ctx'), axis=0)]
  transfers between devices with their start and end apart: 2 -> 2, of which waited for: 2 -> 2; matrix products, arithmetic and copies ran while one was open for 0% -> 1% of each run, Pallas kernels for 0% -> 0%
where the time goes in v1:
time: 321 us; the launch traced here: 320 us
  waiting for transfers between devices  145 us (45%)
  blocking collectives  129 us (40%)
  between operations  15 us (5%)
  matrix products  14.9 us (5%)
  other arithmetic  9.13 us (3%)
  local copies, waits for them, and re-layouts  8.06 us (3%)
    unnamed x3, waiting for transfers between devices  89.5 us
    pmax x1, blocking collectives, local(): largest = lax.pmax(maxima, 'ctx')  57.8 us
    reduce_scatter x1, waiting for transfers between devices, local(): lax.psum_scatter(weighted, 'ctx', scatter_dimension=1, tiled=True)  55.3 us
    all_gather x1, blocking collectives, local(): whole_queries = lax.all_gather(queries, 'ctx', axis=0, tiled=True)  26.4 us
    all_gather x1, blocking collectives, local(): denoms = jnp.sum(lax.all_gather(totals * rescale, 'ctx'), axis=0)  17.8 us
    all_to_all x1, blocking collectives, local(): lax.all_to_all(outgoing, 'ctx', split_axis=0, concat_axis=0, tiled=True)  13.8 us
    all_to_all x1, blocking collectives, local(): lax.all_to_all(expert_out, 'ctx', split_axis=0, concat_axis=0, tiled=True)  12.7 us
  transfers between devices with their start and end apart: 2, of which 2 were waited for; matrix products, arithmetic and copies ran while one was open for 1% of the time, Pallas kernels for 0%

profile of v1, /device:TPU:0, one launch (start us, length us, event | category | flops | bytes accessed | tf_op | source)
XLA Modules:
  0.0 320.5 jit_solution(16930446571297200287)
XLA Ops:
  7.4 1.1 pad_maximum_fusion.1
  8.4 0.7 reshape.88
  9.2 0.9 pad_maximum_fusion
  10.1 0.1 reshape.87
  10.2 26.4 %all-gather.1 = bf16[16,3,4096]{2,1,0:T(4,128)(2,1)} all-gather(bf16[1,3,4096]{2,1,0:T(4,128)(2,1)} %bitcast.59), channel_id=1, replica_groups=mesh['groups'=2,'ctx'=16] {'ctx'}, dimensions={0}, use_global_device_ids=true | all-gather | bytes 417792 | tf_op jit(solution)/shard_map/all_gather | solution.py:35
  36.6 2.2 reshape.89
  38.8 2.7 fusion.47
  41.5 57.8 %pmax.7 = f32[48,32]{0,1:T(8,128)S(1)} all-reduce(f32[48,32]{0,1:T(8,128)S(1)} %bitcast.57), channel_id=1, replica_groups=mesh['groups'=2,'ctx'=16] {'ctx'}, use_global_device_ids=true, to_apply=%region_1.2 | all-reduce | flops 1536 | bytes 12288 | tf_op jit(solution)/shard_map/pmax | solution.py:68
  99.3 2.0 fusion.10
  101.4 0.4 convolution_bitcast_fusion
  101.8 1.1 copy.35
  103.0 17.8 %all-gather.2 = f32[16,48,32]{1,2,0:T(8,128)S(1)} all-gather(f32[1,48,32]{1,2,0:T(8,128)S(1)} %fusion.39), channel_id=2, replica_groups=mesh['groups'=2,'ctx'=16] {'ctx'}, dimensions={0}, use_global_device_ids=true | all-gather | bytes 104448 | tf_op jit(solution)/shard_map/all_gather | solution.py:70
  121.0 0.3 mul.72
  121.2 3.1 bitcast_multiply_fusion
  124.4 0.1 eq.30
  124.5 0.2 convert_reduce_fusion.1
  124.7 0.1 reduce_sum.59
  124.8 55.3 %reduce-scatter.2.cloned.1.call-done = f32[48,256]{1,0:T(8,128)} async-done(((f32[48,4096]{1,0:T(8,128)}), f32[48,256]{1,0:T(8,128)}) %reduce-scatter.2.cloned.1.call-update) | async-done | bytes 49168 | tf_op jit(solution)/shard_map/reduce_scatter | solution.py:72
  180.1 2.3 fusion.37
  182.5 0.6 dynamic-slice
  183.7 0.7 convert_reduce_fusion
  184.4 89.5 %all-reduce.3.cloned.1.call-done = f32[48,2048]{1,0:T(8,128)} async-done(((f32[48,2048]{1,0:T(8,128)}), f32[48,2048]{1,0:T(8,128)}) %all-reduce.3.cloned.1.call-update) | async-done | bytes 393232
  273.9 1.0 multiply_reduce_fusion
  274.9 1.2 convolution_convert_fusion
  276.1 0.8 reshape.93
  276.9 13.8 %all_to_all.10 = bf16[16,3,2048]{2,1,0:T(4,128)(2,1)S(1)} all-to-all(bf16[16,3,2048]{2,1,0:T(4,128)(2,1)} %reshape.93), channel_id=1, replica_groups=mesh['groups'=2,'ctx'=16] {'ctx'}, dimensions={0} | all-to-all | bytes 393216 | tf_op jit(solution)/shard_map/all_to_all | solution.py:101
  290.7 2.6 fusion.4
  293.3 3.9 %fusion.6 = bf16[16,3,2048]{2,0,1:T(8,128)(2,1)} fusion(bf16[1,768,2048]{2,1,0:T(8,128)(2,1)S(1)} %copy-done, bf16[1,2048,768]{2,1,0:T(8,128)(2,1)} %param.24, f32[16,3,768]{2,0,1:T(8,128)S(1)} %fusion.4, bf16[16,3,2048]{2,1,0:T(4,128)(2,1)S(1)} %all_to_all.10), kind=kOutput, calls=%fused_computation.6 | convolution fusion | flops 302309376 | bytes 6832128 | tf_op jit(solution)/shard_map/scf,fd->scd/dot_general | solution.py:107
  297.2 1.1 copy.39
  298.3 12.7 %all_to_all.11 = bf16[16,3,2048]{2,1,0:T(4,128)(2,1)S(1)} all-to-all(bf16[16,3,2048]{2,1,0:T(4,128)(2,1)S(1)} %copy.39), channel_id=1, replica_groups=mesh['groups'=2,'ctx'=16] {'ctx'}, dimensions={0} | all-to-all | bytes 393216 | tf_op jit(solution)/shard_map/all_to_all | solution.py:110
  311.0 0.8 reshape.94
  311.8 1.8 fusion.9
  (28 shorter events, 0.3 us)
Async XLA Ops:
  6.5 286.7 %copy-start = (bf16[1,768,2048]{2,1,0:T(8,128)(2,1)S(1)}, bf16[1,768,2048]{2,1,0:T(8,128)(2,1)}, u32[]{:S(2)}) copy-start(bf16[1,768,2048]{2,1,0:T(8,128)(2,1)} %param.25) | copy-start | bytes 9437188
  6.5 173.6 %reduce-scatter.2.cloned.1.call-start = ((), (), s32[]{:S(2)}) async-start(), calls=%async_computation.3 | async-start | bytes 835584 | tf_op jit(solution)/shard_map/reduce_scatter | solution.py:72
  99.3 2.1 copy-start.1
  121.2 3.2 copy-start.3
  124.3 58.1 %copy-start.4 = (bf16[2048]{0:T(1024)(128)(2,1)S(1)}, bf16[2048]{0:T(1024)(128)(2,1)}, u32[]{:S(2)}) copy-start(bf16[2048]{0:T(1024)(128)(2,1)} %param.22) | copy-start | bytes 12292
  124.3 58.1 %copy-start.6 = (u32[32]{0:T(128)S(1)}, u32[32]{0:T(128)}, u32[]{:S(2)}) copy-start(u32[32]{0:T(128)} %constant.43) | copy-start | bytes 388
  124.3 59.4 %copy-start.5 = (f32[3,8]{1,0:T(4,128)S(1)}, f32[3,8]{1,0:T(4,128)}, u32[]{:S(2)}) copy-start(f32[3,8]{1,0:T(4,128)} %param.27) | copy-start | bytes 292
  124.3 149.5 %copy-start.2 = (bf16[3,2048]{1,0:T(4,128)(2,1)S(1)}, bf16[3,2048]{1,0:T(4,128)(2,1)}, u32[]{:S(2)}) copy-start(bf16[3,2048]{1,0:T(4,128)(2,1)} %param.20) | copy-start | bytes 36868
  124.4 149.5 %all-reduce.3.cloned.1.call-start = ((), (), s32[]{:S(2)}) async-start(), calls=%async_computation.4 | async-start | bytes 786432
Sparse Core Ops, SparseCore 0:
  124.5 55.5 reduce-scatter.1
  183.4 90.3 all-reduce.2
